TPU v7x, 32 devices: a whole 2x2x4 slice. The times are simulated.
32 devices in a mesh: env: 4 (over y, core), dof: 8 (over z, x).
Axes of the slice: x: 2, y: 2, z: 4, core: 2. Of those that a mesh axis runs over, the one named last changes fastest.
Arguments:
- system_matrix: bfloat16 [8, 8192, 8192], P('env', 'dof'), parts along dimension 0, as said below
- forces: float32 [8192, 8, 128], P('dof', 'env'), parts along dimension 1, may hold values from -6 to 6
Outputs:
- accelerations: float32 [8192, 8, 128], P('dof', 'env'), parts along dimension 1
- residual: float32 [8192, 8, 128], P('dof', 'env'), parts along dimension 1
There are 4 independent parts, one for each index of `env`. A program takes and returns all parts, laid end to end along the dimension named above; each array names one. Nothing has to cross between parts.
Inputs may be any that keep to these rules, and one draw needn't show every extreme that they name: `system_matrix`: each environment's matrix is exactly symmetric and positive definite.
All inputs are finite; a program needn't handle non-finite values.
Results may differ from a plain program's by a relative error of at most 0.012.
Values may be sent and summed in bfloat16 or wider, within the bound.
A program may use at most 128 MiB of HBM per device.

v0:
```python
import jax
import jax.numpy as jnp
from jax import lax
from jax.sharding import PartitionSpec as P

ITERS = 4


def apply_matrix(system_matrix, field):
    narrow = field.astype(jnp.bfloat16)
    return jnp.einsum(
        "eic,cer->ier",
        system_matrix,
        lax.all_gather(narrow, "dof", axis=0, tiled=True),
        preferred_element_type=jnp.float32,
    )


def on_device(system_matrix, forces):
    accelerations = jnp.zeros_like(forces)
    residual = forces
    direction = forces
    for step in range(ITERS):
        image = apply_matrix(system_matrix, direction)
        local_sums = (
            jnp.sum(residual * residual, axis=0),
            jnp.sum(direction * image, axis=0),
            jnp.sum(residual * image, axis=0),
            jnp.sum(image * image, axis=0),
        )
        norm_now, curve, cross, square = lax.psum(
            (local_sums[0], local_sums[1], local_sums[2], local_sums[3]), "dof"
        )
        alpha = norm_now / curve
        accelerations = accelerations + alpha * direction
        residual = residual - alpha * image
        norm_next = norm_now - 2.0 * alpha * cross + alpha * alpha * square
        direction = residual + norm_next / norm_now * direction
    return (accelerations, residual)


def solution(mesh):
    placed = (P("env", "dof", None), P("dof", "env", None))
    return jax.shard_map(
        on_device,
        mesh=mesh,
        in_specs=placed,
        out_specs=(P("dof", "env", None), P("dof", "env", None)),
        check_vma=False,
    )
```

profile of v0, /device:TPU:0, one launch (start us, length us, event | category | flops | bytes accessed | tf_op | source)
XLA Modules:
  0.0 467.8 jit_solution(4950738434124669986)
XLA Ops:
  7.2 1.5 copy.5
  8.8 0.9 convert_element_type.12
  9.7 0.0 all-gather.7.cloned.1.call-start
  9.7 1.1 multiply_reduce_fusion.12
  10.8 75.4 %all-gather.5.cloned.1.call-done = bf16[8192,2,128]{0,2,1:T(8,128)(2,1)} async-done(((bf16[1024,2,128]{0,2,1:T(8,128)(2,1)}), bf16[8192,2,128]{0,2,1:T(8,128)(2,1)}) %all-gather.5.cloned.1.call-update) | async-done | bytes 4194320 | tf_op jit(solution)/shard_map/all_gather | solution.py:14
  86.3 17.9 %multiply_reduce_fusion.9 = (f32[2,128]{1,0:T(2,128)S(1)}, f32[2,128]{1,0:T(2,128)S(1)}, f32[1024,2,128]{0,2,1:T(8,128)}) fusion(f32[1024,2,128]{0,2,1:T(8,128)S(1)} %copy.5, bf16[8192,2,128]{0,2,1:T(8,128)(2,1)} %all-gather.5.cloned.1.call-done, bf16[2,1024,8192]{2,1,0:T(8,128)(2,1)} %param.2), kind=kOutput, calls=%fused_computation.20 | convolution fusion | flops 4296015872 | bytes 39847936 | tf_op jit(solution)/shard_map/eic,cer->ier/dot_general | solution.py:11
  104.2 19.0 %all-reduce.3 = (f32[2,128]{1,0:T(2,128)S(1)}, f32[2,128]{1,0:T(2,128)S(1)}, f32[2,128]{1,0:T(2,128)S(1)}) all-reduce(f32[2,128]{1,0:T(2,128)S(1)} %multiply_reduce_fusion.12, f32[2,128]{1,0:T(2,128)S(1)} %get-tuple-element.15, f32[2,128]{1,0:T(2,128)S(1)} %get-tuple-element.14), channel_id=1, replica_groups=mesh['env'=4,'dof'=8] {'dof'}, use_global_device_ids=true, to_apply=%region_1.0 | all-reduce | flops 768 | bytes 6144 | tf_op jit(solution)/shard_map/psum | solution.py:31
  123.1 2.3 fusion.2
  125.5 0.0 all-gather.9.cloned.1.call-start
  125.5 70.1 %all-gather.7.cloned.1.call-done = bf16[8192,2,128]{0,2,1:T(8,128)(2,1)} async-done(((bf16[1024,2,128]{0,2,1:T(8,128)(2,1)}), bf16[8192,2,128]{0,2,1:T(8,128)(2,1)}) %all-gather.7.cloned.1.call-update) | async-done | bytes 4194320 | tf_op jit(solution)/shard_map/all_gather | solution.py:14
  195.6 18.0 %multiply_reduce_fusion.6 = (f32[2,128]{1,0:T(2,128)S(1)}, f32[2,128]{1,0:T(2,128)S(1)}, f32[2,128]{1,0:T(2,128)S(1)}, f32[2,128]{1,0:T(2,128)S(1)}, f32[1024,2,128]{0,2,1:T(8,128)}) fusion(f32[1024,2,128]{0,2,1:T(8,128)S(1)} %get-tuple-element.40, f32[1024,2,128]{0,2,1:T(8,128)S(1)} %get-tuple-element.39, ...), kind=kOutput, calls=%fused_computation.15 | convolution fusion | flops 4297064448 | bytes 40898560 | tf_op jit(solution)/shard_map/eic,cer->ier/dot_general | solution.py:11
  213.7 19.0 %all-reduce.2 = (f32[2,128]{1,0:T(2,128)S(1)}, f32[2,128]{1,0:T(2,128)S(1)}, f32[2,128]{1,0:T(2,128)S(1)}, f32[2,128]{1,0:T(2,128)S(1)}) all-reduce(f32[2,128]{1,0:T(2,128)S(1)} %get-tuple-element.13, f32[2,128]{1,0:T(2,128)S(1)} %get-tuple-element.12, f32[2,128]{1,0:T(2,128)S(1)} %get-tuple-element.11, ...), channel_id=1, replica_groups=mesh['env'=4,'dof'=8] {'dof'}, use_global_device_ids=true, to_apply=%region_5.0 | all-reduce | flops 1024 | bytes 8192 | tf_op jit(solution)/shard_map/psum | solution.py:31
  232.7 3.0 fusion.1
  235.6 0.0 all-gather.11.cloned.1.call-start
  235.7 70.1 %all-gather.9.cloned.1.call-done = bf16[8192,2,128]{0,2,1:T(8,128)(2,1)} async-done(((bf16[1024,2,128]{0,2,1:T(8,128)(2,1)}), bf16[8192,2,128]{0,2,1:T(8,128)(2,1)}) %all-gather.9.cloned.1.call-update) | async-done | bytes 4194320 | tf_op jit(solution)/shard_map/all_gather | solution.py:14
  305.8 18.3 %multiply_reduce_fusion.2 = (f32[2,128]{1,0:T(2,128)S(1)}, f32[2,128]{1,0:T(2,128)S(1)}, f32[2,128]{1,0:T(2,128)S(1)}, f32[2,128]{1,0:T(2,128)S(1)}, f32[1024,2,128]{0,2,1:T(8,128)}) fusion(f32[1024,2,128]{0,2,1:T(8,128)} %get-tuple-element.35, f32[1024,2,128]{0,2,1:T(8,128)S(1)} %get-tuple-element.34, ...), kind=kOutput, calls=%fused_computation.9 | convolution fusion | flops 4297064448 | bytes 40898560 | tf_op jit(solution)/shard_map/eic,cer->ier/dot_general | solution.py:11
  324.1 19.0 %all-reduce.1 = (f32[2,128]{1,0:T(2,128)S(1)}, f32[2,128]{1,0:T(2,128)S(1)}, f32[2,128]{1,0:T(2,128)S(1)}, f32[2,128]{1,0:T(2,128)S(1)}) all-reduce(f32[2,128]{1,0:T(2,128)S(1)} %get-tuple-element.9, f32[2,128]{1,0:T(2,128)S(1)} %get-tuple-element.8, f32[2,128]{1,0:T(2,128)S(1)} %get-tuple-element.7, ...), channel_id=1, replica_groups=mesh['env'=4,'dof'=8] {'dof'}, use_global_device_ids=true, to_apply=%region_11.0 | all-reduce | flops 1024 | bytes 8192 | tf_op jit(solution)/shard_map/psum | solution.py:31
  343.0 2.9 fusion
  346.0 70.2 %all-gather.11.cloned.1.call-done = bf16[8192,2,128]{0,2,1:T(8,128)(2,1)} async-done(((bf16[1024,2,128]{0,2,1:T(8,128)(2,1)}), bf16[8192,2,128]{0,2,1:T(8,128)(2,1)}) %all-gather.11.cloned.1.call-update) | async-done | bytes 4194320 | tf_op jit(solution)/shard_map/all_gather | solution.py:14
  416.2 18.3 %multiply_reduce_fusion = (f32[2,128]{1,0:T(2,128)S(1)}, f32[2,128]{1,0:T(2,128)S(1)}, f32[1024,2,128]{0,2,1:T(8,128)}) fusion(f32[1024,2,128]{0,2,1:T(8,128)} %get-tuple-element.30, f32[1024,2,128]{0,2,1:T(8,128)S(1)} %get-tuple-element.34, f32[2,128]{1,0:T(2,128)S(1)} %get-tuple-element.31, bf16[8192,2,128]{0,2,1:T(8,128)(2,1)} %all-gather.11.cloned.1.call-done, ...), kind=kOutput, calls=%fused_computation.6 | convolution fusion | flops 4296540160 | bytes 40897536 | tf_op jit(solution)/shard_map/eic,cer->ier/dot_general | solution.py:11
  434.4 19.0 %all-reduce = (f32[2,128]{1,0:T(2,128)S(1)}, f32[2,128]{1,0:T(2,128)S(1)}) all-reduce(f32[2,128]{1,0:T(2,128)S(1)} %get-tuple-element.5, f32[2,128]{1,0:T(2,128)S(1)} %get-tuple-element.4), channel_id=1, replica_groups=mesh['env'=4,'dof'=8] {'dof'}, use_global_device_ids=true, to_apply=%region_19.0 | all-reduce | flops 512 | bytes 4096 | tf_op jit(solution)/shard_map/psum | solution.py:31
  453.4 3.4 multiply_subtract_fusion
  456.8 2.2 copy.10
  459.0 2.2 copy.9
  (13 shorter events, 0.2 us)
Async XLA Ops:
  7.2 2.6 copy-start.1
  7.2 79.1 %all-gather.5.cloned.1.call-start = ((), (), s32[]{:S(2)}) async-start(), calls=%async_computation | async-start | bytes 4718592 | tf_op jit(solution)/shard_map/all_gather | solution.py:14
  9.7 185.9 %all-gather.7.cloned.1.call-start = ((), (), s32[]{:S(2)}) async-start(), calls=%async_computation.1 | async-start | bytes 4718592 | tf_op jit(solution)/shard_map/all_gather | solution.py:14
  125.4 88.2 %copy-start = (f32[1024,2,128]{0,2,1:T(8,128)}, f32[1024,2,128]{0,2,1:T(8,128)S(1)}, u32[]{:S(2)}) copy-start(f32[1024,2,128]{0,2,1:T(8,128)S(1)} %get-tuple-element.40) | copy-start | bytes 3145732
  125.5 180.3 %all-gather.9.cloned.1.call-start = ((), (), s32[]{:S(2)}) async-start(), calls=%async_computation.2 | async-start | bytes 4718592 | tf_op jit(solution)/shard_map/all_gather | solution.py:14
  235.6 180.5 %all-gather.11.cloned.1.call-start = ((), (), s32[]{:S(2)}) async-start(), calls=%async_computation.3 | async-start | bytes 4718592 | tf_op jit(solution)/shard_map/all_gather | solution.py:14
Sparse Core Ops, SparseCore 0:
  10.7 75.4 all-gather.4
  125.6 69.9 all-gather.6
  235.8 69.9 all-gather.8
  346.1 69.9 all-gather.10
where the time goes:
time: 468 us
  waiting for transfers between devices  286 us (61%)
  blocking collectives  75.9 us (16%)
  matrix products  72.5 us (15%)
  between operations  13.8 us (3%)
  other arithmetic  13.6 us (3%)
  local copies, waits for them, and re-layouts  6.04 us (1%)
    all_gather x4, waiting for transfers between devices, apply_matrix(): lax.all_gather(narrow, 'dof', axis=0, tiled=True)  286 us
    psum x4, blocking collectives, on_device(): lax.psum((local_sums[0], local_sums[1], local_sums[2], local_sums[3]), 'd...  75.9 us
    dot_general x4, matrix products, apply_matrix(): jnp.einsum('eic,cer->ier', system_matrix, lax.all_gather(narrow, 'dof', a...  72.5 us
  transfers between devices with their start and end apart: 4, of which 4 were waited for; matrix products, arithmetic and copies ran while one was open for 0% of the time, Pallas kernels for 0%

commit v1 on v0

v1 whole, which is shorter than its diff:
```python
import functools

import jax
import jax.numpy as jnp
from jax import lax
from jax.experimental import pallas as pl
from jax.experimental.pallas import tpu as pltpu
from jax.sharding import PartitionSpec as P

ITERS = 4
MESH = pl.DeviceIdType.MESH


def ring_order(n):
    width = 1
    while (2 * width) ** 2 <= n:
        width *= 2
    depth = n // width
    if width == 1 or depth % 2:
        return list(range(n))
    order = [z * width for z in range(depth)]
    for turn, z in enumerate(reversed(range(depth))):
        xs = list(range(1, width))
        order += [z * width + x for x in (xs if turn % 2 == 0 else xs[::-1])]
    return order


def lookup(table, index):
    value = jnp.int32(0)
    for place, entry in enumerate(table):
        value = value + jnp.where(index == place, jnp.int32(entry), jnp.int32(0))
    return value


def kernel(n, envs, rows, a_hbm, f_ref, x_ref, r_ref, a_vmem, field, direction, image, sums,
           load_sem, send_sem, recv_sem, sum_send, sum_recv):
    order = ring_order(n)
    inverse = [order.index(i) for i in range(n)]
    me = lax.axis_index("dof")
    place = lookup(inverse, me)
    half = rows // 2
    far = n // 2
    tile = min(128, rows)

    def owner(step):
        return lookup(order, lax.rem(place + step + n, n))

    following, previous = owner(1), owner(-1)

    def load(env, block):
        return pltpu.make_async_copy(
            a_hbm.at[env, :, pl.ds(pl.multiple_of(block * rows, rows), rows)],
            a_vmem.at[env, block],
            load_sem.at[env, block],
        )

    def hop(env, way, block, part, target):
        return pltpu.make_async_remote_copy(
            src_ref=field.at[env, block, part],
            dst_ref=field.at[env, block, part],
            send_sem=send_sem.at[env, way, block, part],
            recv_sem=recv_sem.at[env, block, part],
            device_id={"dof": target},
            device_id_type=MESH,
        )

    def forward(env, block, part):
        return hop(env, 0, block, part, following)

    def backward(env, block, part):
        return hop(env, 1, block, part, previous)

    def share(env, slot, peer, source):
        return pltpu.make_async_remote_copy(
            src_ref=sums.at[env, slot, source],
            dst_ref=sums.at[env, slot, source],
            send_sem=sum_send.at[env, slot, peer],
            recv_sem=sum_recv.at[env, slot, source],
            device_id={"dof": peer},
            device_id_type=MESH,
        )

    def peer_of(j):
        return lax.rem(me + j, n)

    def add(env, block, part, first=False):
        product = jnp.dot(
            a_vmem[env, block, :, part * half:(part + 1) * half],
            field[env, block, part],
            preferred_element_type=jnp.float32,
        )
        if first:
            image[env] = product
        else:
            image[env] += product

    def start_own(env):
        for q in range(2):
            forward(env, me, q).start()
            backward(env, me, 1 - q).start()

    def begin(env, k):
        @pl.when(k == 0)
        def _():
            load(env, me).wait()
        add(env, me, 0, first=True)
        add(env, me, 1)

    def near(env, k, s, relay):
        before, after = owner(-s), owner(s)
        for q in range(2):
            forward(env, before, q).wait_recv()
            if relay > q:
                forward(env, before, q).start()
            backward(env, after, 1 - q).wait_recv()
            if relay > q:
                backward(env, after, 1 - q).start()
            if q == 0:
                @pl.when(k == 0)
                def _():
                    load(env, before).wait()
                    load(env, after).wait()
            if relay == 1 and q == 0:
                yield
            add(env, before, q)
            add(env, after, 1 - q)

    def gather(env, k, between):
        begin(env, k)

        def step(s, carry):
            for _ in near(env, k, s, 2):
                pass
            return carry

        lax.fori_loop(1, far - 1, step, 0)
        for _ in near(env, k, far - 1, 1):
            between()
        block = owner(far)
        forward(env, block, 0).wait_recv()

        @pl.when(k == 0)
        def _():
            load(env, block).wait()
        add(env, block, 0)
        backward(env, block, 1).wait_recv()
        add(env, block, 1)

        def drain(s, carry):
            for q in range(2):
                forward(env, owner(-s), q).wait_send()
                backward(env, owner(s), q).wait_send()
            return carry

        lax.fori_loop(0, far - 1, drain, 0)
        forward(env, owner(1 - far), 0).wait_send()
        backward(env, owner(far - 1), 1).wait_send()

    def local_sums(env, k):
        slot = lax.rem(k, 2)

        def step(i, carry):
            at = pl.ds(pl.multiple_of(i * tile, tile), tile)
            r, d, q = r_ref[env, at, :], direction[env, at, :], image[env, at, :]
            fold = lambda v: jnp.sum(v.reshape(tile // 8, 8, v.shape[-1]), axis=0)
            return tuple(c + fold(v) for c, v in zip(carry, (r * r, d * q, r * q, q * q)))

        zero = jnp.zeros((8, image.shape[-1]), jnp.float32)
        totals = lax.fori_loop(0, rows // tile, step, (zero,) * 4)
        for i, total in enumerate(totals):
            sums[env, slot, me, i:i + 1, :] = jnp.sum(total, axis=0, keepdims=True)

        def send(j, carry):
            share(env, slot, peer_of(j), me).start()
            return carry

        lax.fori_loop(1, n, send, 0)

    def update(env, k):
        slot = lax.rem(k, 2)

        def receive(j, carry):
            share(env, slot, me, peer_of(j)).wait_recv()
            share(env, slot, peer_of(j), me).wait_send()
            return carry

        lax.fori_loop(1, n, receive, 0)
        total = sums[env, slot, 0]
        for j in range(1, n):
            total = total + sums[env, slot, j]
        now, curve, cross, square = (total[i:i + 1, :] for i in range(4))
        alpha = now / curve
        beta = (now - 2.0 * alpha * cross + alpha * alpha * square) / now

        def step(i, carry):
            at = pl.ds(pl.multiple_of(i * tile, tile), tile)
            d = direction[env, at, :]
            x_ref[env, at, :] = x_ref[env, at, :] + alpha * d
            r = r_ref[env, at, :] - alpha * image[env, at, :]
            r_ref[env, at, :] = r
            d = r + beta * d
            direction[env, at, :] = d
            put(env, i, d)
            return carry

        lax.fori_loop(0, rows // tile, step, 0)

    def put(env, i, d):
        per = half // tile if half >= tile else 1
        narrow = d.astype(field.dtype)
        if half >= tile:
            at = pl.ds(pl.multiple_of(lax.rem(i, per) * tile, tile), tile)
            field[env, me, i // per, at, :] = narrow
        else:
            for q in range(2):
                field[env, me, q] = narrow[q * half:(q + 1) * half]

    barrier = pltpu.get_barrier_semaphore()

    def greet(j, carry):
        pl.semaphore_signal(barrier, inc=1, device_id={"dof": peer_of(j)}, device_id_type=MESH)
        return carry

    def copy_in(env):
        def step(i, carry):
            at = pl.ds(pl.multiple_of(i * tile, tile), tile)
            f = f_ref[env, at, :]
            x_ref[env, at, :] = jnp.zeros_like(f)
            r_ref[env, at, :] = f
            direction[env, at, :] = f
            put(env, i, f)
            return carry
        lax.fori_loop(0, rows // tile, step, 0)

    lax.fori_loop(1, n, greet, 0)
    copy_in(0)
    for env in range(envs):
        load(env, me).start()

        def fetch(s, carry):
            load(env, owner(-s)).start()
            load(env, owner(s)).start()
            return carry

        lax.fori_loop(1, far, fetch, 0)
        load(env, owner(far)).start()
    pl.semaphore_wait(barrier, n - 1)
    start_own(0)
    copy_in(1)

    def iteration(k, carry):
        def second():
            @pl.when(k > 0)
            def _():
                update(1, k - 1)
            start_own(1)

        def first():
            update(0, k)

            @pl.when(k < ITERS - 1)
            def _():
                start_own(0)

        gather(0, k, second)
        local_sums(0, k)
        gather(1, k, first)
        local_sums(1, k)
        return carry

    lax.fori_loop(0, ITERS, iteration, 0)
    update(1, ITERS - 1)


def solution(mesh):
    n = mesh.shape["dof"]

    def on_device(system_matrix, forces):
        envs, rows, _ = system_matrix.shape
        rhs = forces.shape[-1]
        block = jax.ShapeDtypeStruct((envs, rows, rhs), jnp.float32)
        vmem = pl.BlockSpec(memory_space=pltpu.VMEM)
        x, r = pl.pallas_call(
            functools.partial(kernel, n, envs, rows),
            out_shape=(block, block),
            in_specs=[pl.BlockSpec(memory_space=pl.ANY), vmem],
            out_specs=(vmem, vmem),
            scratch_shapes=[
                pltpu.VMEM((envs, n, rows, rows), jnp.bfloat16),
                pltpu.VMEM((envs, n, 2, rows // 2, rhs), jnp.bfloat16),
                pltpu.VMEM((envs, rows, rhs), jnp.float32),
                pltpu.VMEM((envs, rows, rhs), jnp.float32),
                pltpu.VMEM((envs, 2, n, 4, rhs), jnp.float32),
                pltpu.SemaphoreType.DMA((envs, n)),
                pltpu.SemaphoreType.DMA((envs, 2, n, 2)),
                pltpu.SemaphoreType.DMA((envs, n, 2)),
                pltpu.SemaphoreType.DMA((envs, 2, n)),
                pltpu.SemaphoreType.DMA((envs, 2, n)),
            ],
            compiler_params=pltpu.CompilerParams(
                collective_id=0, has_side_effects=True, vmem_limit_bytes=60 * 1024 * 1024
            ),
        )(system_matrix, forces.transpose(1, 0, 2))
        return x.transpose(1, 0, 2), r.transpose(1, 0, 2)

    return jax.shard_map(
        on_device,
        mesh=mesh,
        in_specs=(P("env", "dof", None), P("dof", "env", None)),
        out_specs=(P("dof", "env", None), P("dof", "env", None)),
        check_vma=False,
    )
```

time: 468 us -> 185 us (0.40)
  waiting for transfers between devices: 286 us -> 0 us
  Pallas kernels: 0 us -> 176 us
  blocking collectives: 75.9 us -> 0 us
  matrix products: 72.5 us -> 0 us
  other arithmetic: 13.6 us -> 0 us
  between operations: 13.8 us -> 0.64 us
    all_gather x4 -> x0, waiting for transfers between devices: 286 us -> none  [apply_matrix(): lax.all_gather(narrow, 'dof', axis=0, tiled=True)]
    pallas_call x0 -> x1, Pallas kernels: none -> 176 us  [on_device(): pl.pallas_call(functools.partial(kernel, n, envs, rows), out_shape=(block...]
    psum x4 -> x0, blocking collectives: 75.9 us -> none  [on_device(): lax.psum((local_sums[0], local_sums[1], local_sums[2], local_sums[3]), 'd...]
    dot_general x4 -> x0, matrix products: 72.5 us -> none  [apply_matrix(): jnp.einsum('eic,cer->ier', system_matrix, lax.all_gather(narrow, 'dof', a...]
    convert_element_type x4 -> x0, other arithmetic: 9.05 us -> none  [apply_matrix(): narrow = field.astype(jnp.bfloat16)]
  transfers between devices with their start and end apart: 4 -> 0, of which waited for: 4 -> 0; matrix products, arithmetic and copies ran while one was open for 0% -> 0% of each run, Pallas kernels for 0% -> 0%
where the time goes in v1:
time: 185 us
  Pallas kernels  176 us (95%)
  local copies, waits for them, and re-layouts  8.27 us (4%)
    pallas_call x1, Pallas kernels, on_device(): pl.pallas_call(functools.partial(kernel, n, envs, rows), out_shape=(block...  176 us
    unnamed x3, local copies, waits for them, and re-layouts  8.27 us

profile of v1, /device:TPU:0, one launch (start us, length us, event | category | flops | bytes accessed | tf_op | source)
XLA Modules:
  0.0 184.7 jit_solution(15022841667054797928)
XLA Ops:
  0.6 2.3 %copy.8 = f32[1024,2,128]{2,0,1:T(8,128)} copy(f32[1024,2,128]{2,1,0:T(2,128)} %param.3) | data formatting | bytes 2097152 | tf_op args[1]
  2.9 175.8 %shard_map.41 = (f32[2,1024,128]{2,1,0:T(8,128)}, f32[2,1024,128]{2,1,0:T(8,128)}) custom-call(bf16[2,1024,8192]{2,1,0:T(8,128)(2,1)} %a_hbm.1, f32[2,1024,128]{2,1,0:T(8,128)} %bitcast.5), custom_call_target="tpu_custom_call" | custom-call | tf_op jit(solution)/shard_map/pallas_call | solution.py:283
  178.7 3.0 %copy.5 = f32[1024,2,128]{2,1,0:T(2,128)} copy(f32[1024,2,128]{2,0,1:T(8,128)} %bitcast.7) | data formatting | bytes 2097152
  181.7 3.0 %copy.6 = f32[1024,2,128]{2,1,0:T(2,128)} copy(f32[1024,2,128]{2,0,1:T(8,128)} %bitcast.6) | data formatting | bytes 2097152
